TPU v7x, 32 devices: a whole 2x2x4 slice. The times are simulated.
32 devices in a mesh: grow: 8 (over y, x, core), gcol: 4 (over z).
Axes of the slice: x: 2, y: 2, z: 4, core: 2. Of those that a mesh axis runs over, the one named last changes fastest.
Arguments:
- eps_static: float32 [12288, 12288], P('grow', 'gcol'), may hold values from -1.8 to 1.8
- eps_imag: float32 [12288, 12288], P('grow', 'gcol'), may hold values from -1.8 to 1.8
- frequency_grid: float32 [3], replicated, may hold values from 0.1 to 2
- band_energy: float32 [32], replicated, may hold values from -2 to 2
- pair_elements: bfloat16 [32, 64, 12288], P('grow', None, 'gcol'), may hold values from -0.0546875 to 0.0546875
Outputs:
- sigma: float32 [3, 64], P(None, 'gcol')
All inputs are finite; a program needn't handle non-finite values.
Results may differ from a plain program's by a relative error of at most 0.0019.
Values may be sent and summed in bfloat16 or wider, within the bound.
A program may use at most 128 MiB of HBM per device.

v0:
```python
import jax
import jax.numpy as jnp
from jax import lax
from jax.sharding import PartitionSpec as P

NE = 3


def broadcast(block, axis, owner):
    block = jnp.where(lax.axis_index(axis) == owner, block, jnp.zeros_like(block))
    return lax.psum(block, axis)


def shards(eps_static, eps_imag, frequency_grid, band_energy, pair_elements):
    row_count = lax.axis_size("grow")
    col_count = lax.axis_size("gcol")
    group_ratio = row_count // col_count
    row_index = lax.axis_index("grow")
    col_index = lax.axis_index("gcol")
    height = eps_static.shape[0]
    breadth = eps_static.shape[1]
    bands = pair_elements.shape[0] * row_count
    states = pair_elements.shape[1]
    column_panel = lax.all_gather(pair_elements, "grow", axis=0, tiled=True)
    offset = row_index % group_ratio * height
    section = lax.dynamic_slice_in_dim(column_panel, offset, height, 2)
    row_panel = broadcast(section, "gcol", row_index // group_ratio)
    global_rows = row_index * height + lax.iota(jnp.int32, height)
    global_cols = col_index * breadth + lax.iota(jnp.int32, breadth)
    kronecker = (global_rows[:, None] == global_cols[None, :]).astype(jnp.float32)
    static_part = eps_static - kronecker
    imag_part = eps_imag - kronecker
    spread = static_part - imag_part
    pole_square = (imag_part * imag_part + 0.25) / (spread * spread + 0.25)
    pole_freq = jnp.sqrt(pole_square)
    strength = -static_part * pole_square
    left_rows = row_panel.reshape(bands * states, height)
    right_rows = column_panel.reshape(bands * states, breadth)
    terms = []
    for point in range(NE):
        kernel = (strength / (pole_freq * (pole_freq + frequency_grid[point]))).astype(jnp.bfloat16)
        projected = jnp.dot(left_rows, kernel, preferred_element_type=jnp.float32)
        terms.append(jnp.sum(projected * right_rows, axis=1))
    quad = jnp.stack(terms).reshape(NE, bands, states)
    offset_energy = frequency_grid[:, None] - band_energy[None, :]
    weight = 1.0 / (1.0 + offset_energy * offset_energy)
    partial_sigma = jnp.einsum("em,ems->es", weight, quad)
    shares = lax.psum_scatter(partial_sigma, "gcol", scatter_dimension=1, tiled=True)
    return lax.psum(shares, "grow")


def solution(mesh):
    return jax.shard_map(
        shards,
        mesh=mesh,
        in_specs=(P("grow", "gcol"), P("grow", "gcol"), P(), P(), P("grow", None, "gcol")),
        out_specs=P(None, "gcol"),
        check_vma=False,
    )
```

profile of v0, /device:TPU:0, one launch (start us, length us, event | category | flops | bytes accessed | tf_op | source)
XLA Modules:
  0.0 466.5 jit_solution(14416005977616240631)
XLA Ops:
  6.5 0.0 copy-start.1
  6.5 0.0 copy-start.3
  6.5 0.0 all-gather.2.cloned.1.call-start
  6.5 0.7 all-gather.2.cloned.1.call-update
  7.3 0.0 all-reduce.2.cloned.1.call-start
  7.3 76.6 %all-gather.2.cloned.1.call-done = bf16[32,64,3072]{2,1,0:T(8,128)(2,1)} async-done(((bf16[4,64,3072]{2,1,0:T(8,128)(2,1)}), bf16[32,64,3072]{2,1,0:T(8,128)(2,1)}) %all-gather.2.cloned.1.call-update) | async-done | bytes 12582928 | tf_op jit(solution)/shard_map/all_gather | solution.py:24
  84.0 6.9 %dynamic-slice_select_fusion = bf16[32,64,1536]{2,1,0:T(8,128)(2,1)} fusion(bf16[32,64,3072]{2,1,0:T(8,128)(2,1)} %all-gather.2.cloned.1.call-done, s32[]{:T(128)S(6)} %select_n.25, pred[]{:T(512)S(6)} %eq.18), kind=kLoop, calls=%fused_computation.19 | loop fusion | flops 3145728 | bytes 12582917 | tf_op jit(solution)/shard_map/jit(_where)/select_n | solution.py:10
  90.9 0.0 all-reduce.2.cloned.1.call-update
  90.9 0.0 reduce-scatter.4.cloned.1.call-start
  90.9 0.0 copy-done.1
  91.0 0.6 fusion.20
  91.6 0.0 copy-done.3
  91.6 0.6 divide_bitcast_fusion
  92.2 221.7 %all-reduce.2.cloned.1.call-done = bf16[2048,1536]{1,0:T(8,128)(2,1)} async-done(((bf16[2048,1536]{1,0:T(8,128)(2,1)}), bf16[2048,1536]{1,0:T(8,128)(2,1)}) %all-reduce.2.cloned.1.call-update) | async-done | bytes 6291472 | tf_op jit(solution)/shard_map/psum | solution.py:11
  313.9 37.5 %fusion = bf16[2048]{0:T(1024)(128)(2,1)S(1)} fusion(bf16[2048,3072]{1,0:T(8,128)(2,1)} %bitcast.17, bf16[2048,1536]{1,0:T(8,128)(2,1)} %all-reduce.2.cloned.1.call-done, f32[]{:T(128)} %bitcast.2, f32[1536,3072]{1,0:T(8,128)} %param.5, s32[3072]{0:T(1024)S(1)} %iota_add_fusion, s32[1536]{0:T(1024)S(1)} %iota_add_fusion.1, f32[1536,3072]{1,0:T(8,128)} %param.6), kind=kOutput, calls=%fused_computation.8 | convolution fusion | flops 19421722624 | bytes 56645636 | tf_op jit(solution)/shard_map/dot_general | solution.py:42
  351.4 0.7 stack.12
  352.1 37.6 %fusion.1 = bf16[2048]{0:T(1024)(128)(2,1)S(1)} fusion(bf16[2048,3072]{1,0:T(8,128)(2,1)} %bitcast.18, bf16[2048,1536]{1,0:T(8,128)(2,1)} %all-reduce.2.cloned.1.call-done, f32[]{:T(128)} %bitcast.4, f32[1536,3072]{1,0:T(8,128)} %param.5, s32[3072]{0:T(1024)S(1)} %iota_add_fusion, s32[1536]{0:T(1024)S(1)} %iota_add_fusion.1, f32[1536,3072]{1,0:T(8,128)} %param.6), kind=kOutput, calls=%fused_computation.9 | convolution fusion | flops 19421722624 | bytes 56645636 | tf_op jit(solution)/shard_map/dot_general | solution.py:42
  389.7 0.1 stack.13
  389.8 0.0 copy-start
  389.8 0.0 copy-start.2
  389.8 37.7 %fusion.2 = bf16[2048]{0:T(1024)(128)(2,1)S(1)} fusion(bf16[2048,3072]{1,0:T(8,128)(2,1)} %bitcast.19, bf16[2048,1536]{1,0:T(8,128)(2,1)} %all-reduce.2.cloned.1.call-done, f32[]{:T(128)} %bitcast.6, f32[1536,3072]{1,0:T(8,128)} %param.5, s32[3072]{0:T(1024)S(1)} %iota_add_fusion, s32[1536]{0:T(1024)S(1)} %iota_add_fusion.1, f32[1536,3072]{1,0:T(8,128)} %param.6), kind=kOutput, calls=%fused_computation.10 | convolution fusion | flops 19421722624 | bytes 56645636 | tf_op jit(solution)/shard_map/dot_general | solution.py:42
  427.5 0.1 stack.14
  427.6 0.0 copy-done
  427.6 0.0 copy-done.2
  427.6 0.1 fusion.12
  427.8 0.7 copy.8
  428.5 0.0 reduce-scatter.4.cloned.1.call-update
  428.5 18.3 %reduce-scatter.4.cloned.1.call-done = f32[16,3]{1,0:T(8,128)} async-done(((f32[64,3]{1,0:T(8,128)}), f32[16,3]{1,0:T(8,128)}) %reduce-scatter.4.cloned.1.call-update) | async-done | bytes 208
  446.8 0.8 copy.9
  447.6 12.4 %psum.15 = f32[3,16]{1,0:T(4,128)} all-reduce(f32[3,16]{1,0:T(4,128)S(1)} %copy.9), channel_id=1, replica_groups=mesh['grow'=8,'gcol'=4] {'grow'}, use_global_device_ids=true, to_apply=%region_5.6 | all-reduce | flops 48 | bytes 384 | tf_op jit(solution)/shard_map/psum | solution.py:49
  (3 shorter events, 0.0 us)
Async XLA Ops:
  6.5 84.4 %copy-start.1 = (f32[3]{0:T(128)S(1)}, f32[3]{0:T(128)}, u32[]{:S(2)}) copy-start(f32[3]{0:T(128)} %param.7) | copy-start | bytes 40
  6.5 85.0 %copy-start.3 = (f32[32]{0:T(128)S(1)}, f32[32]{0:T(128)}, u32[]{:S(2)}) copy-start(f32[32]{0:T(128)} %param.8) | copy-start | bytes 388
  6.5 77.4 %all-gather.2.cloned.1.call-start = ((), (), s32[]{:S(2)}) async-start(), calls=%async_computation.1 | async-start | bytes 14155776 | tf_op jit(solution)/shard_map/all_gather | solution.py:24
  7.3 306.6 %all-reduce.2.cloned.1.call-start = ((), (), s32[]{:S(2)}) async-start(), calls=%async_computation.2 | async-start | bytes 12582912 | tf_op jit(solution)/shard_map/psum | solution.py:11
  90.9 355.9 %reduce-scatter.4.cloned.1.call-start = ((), (), s32[]{:S(2)}) async-start(), calls=%async_computation.3 | async-start | bytes 40960
  389.8 37.8 %copy-start = (bf16[1,32,64]{2,1,0:T(8,128)(2,1)S(1)}, bf16[1,32,64]{2,1,0:T(8,128)(2,1)}, u32[]{:S(2)}) copy-start(bf16[1,32,64]{2,1,0:T(8,128)(2,1)} %stack.12) | copy-start | bytes 12292
  389.8 37.8 %copy-start.2 = (bf16[3,32,1]{1,0,2:T(4,128)(2,1)S(1)}, bf16[3,32,1]{1,0,2:T(4,128)(2,1)}, u32[]{:S(2)}) copy-start(bf16[3,32,1]{1,0,2:T(4,128)(2,1)} %divide_bitcast_fusion) | copy-start | bytes 580
Sparse Core Ops, SparseCore 0:
  9.2 74.7 all-gather.1
  91.0 222.8 all-reduce.1
  428.6 18.1 reduce-scatter.3
where the time goes:
time: 467 us; the launch traced here: 466 us
  waiting for transfers between devices  317 us (68%)
  matrix products  113 us (24%)
  between operations  13.2 us (3%)
  blocking collectives  12.4 us (3%)
  other arithmetic  7.55 us (2%)
    psum x1, waiting for transfers between devices, broadcast(): return lax.psum(block, axis)  222 us
    dot_general x3, matrix products, shards(): projected = jnp.dot(left_rows, kernel, preferred_element_type=jnp.float32)  113 us
    all_gather x1, waiting for transfers between devices, shards(): column_panel = lax.all_gather(pair_elements, 'grow', axis=0, tiled=True)  76.6 us
    unnamed x4, waiting for transfers between devices  19 us
    psum x1, blocking collectives, shards(): return lax.psum(shares, 'grow')  12.4 us
  transfers between devices with their start and end apart: 3, of which 3 were waited for; matrix products, arithmetic and copies ran while one was open for 0% of the time, Pallas kernels for 0%

commit v1 on v0

--- a/solution.py
+++ b/solution.py
@@ -8,7 +8,7 @@
 
 def broadcast(block, axis, owner):
     block = jnp.where(lax.axis_index(axis) == owner, block, jnp.zeros_like(block))
-    return lax.psum(block, axis)
+    return jnp.sum(lax.all_gather(block, axis), axis=0)
 
 
 def shards(eps_static, eps_imag, frequency_grid, band_energy, pair_elements):

time: 467 us -> 686 us (1.47)
  waiting for transfers between devices: 317 us -> 519 us
  other arithmetic: 7.55 us -> 25.3 us
    all_gather x0 -> x1, waiting for transfers between devices: none -> 424 us  [broadcast(): return jnp.sum(lax.all_gather(block, axis), axis=0)]
    psum x1 -> x0, waiting for transfers between devices: 222 us -> none  [broadcast(): return lax.psum(block, axis)]
    reduce_sum x0 -> x1, other arithmetic: none -> 17.7 us  [broadcast(): return jnp.sum(lax.all_gather(block, axis), axis=0)]
where the time goes in v1:
time: 686 us
  waiting for transfers between devices  519 us (76%)
  matrix products  113 us (16%)
  other arithmetic  25.3 us (4%)
  between operations  13.2 us (2%)
  blocking collectives  12.4 us (2%)
    all_gather x1, waiting for transfers between devices, broadcast(): return jnp.sum(lax.all_gather(block, axis), axis=0)  424 us
    dot_general x3, matrix products, shards(): projected = jnp.dot(left_rows, kernel, preferred_element_type=jnp.float32)  113 us
    all_gather x1, waiting for transfers between devices, shards(): column_panel = lax.all_gather(pair_elements, 'grow', axis=0, tiled=True)  76.6 us
    unnamed x4, waiting for transfers between devices  18.3 us
    reduce_sum x1, other arithmetic, broadcast(): return jnp.sum(lax.all_gather(block, axis), axis=0)  17.7 us
  transfers between devices with their start and end apart: 3, of which 3 were waited for; matrix products, arithmetic and copies ran while one was open for 0% of the time, Pallas kernels for 0%

profile of v1, /device:TPU:0, one launch (start us, length us, event | category | flops | bytes accessed | tf_op | source)
XLA Modules:
  0.0 685.9 jit_solution(10765311253451768482)
XLA Ops:
  6.5 0.0 copy-start.1
  6.5 0.0 copy-start.3
  6.5 0.0 all-gather.4.cloned.1.call-start
  6.5 0.7 all-gather.4.cloned.1.call-update
  7.3 0.0 all-gather.6.cloned.1.call-start
  7.3 76.6 %all-gather.4.cloned.1.call-done = bf16[32,64,3072]{2,1,0:T(8,128)(2,1)} async-done(((bf16[4,64,3072]{2,1,0:T(8,128)(2,1)}), bf16[32,64,3072]{2,1,0:T(8,128)(2,1)}) %all-gather.4.cloned.1.call-update) | async-done | bytes 12582928 | tf_op jit(solution)/shard_map/all_gather | solution.py:24
  84.0 6.9 %dynamic-slice_select_fusion = bf16[32,64,1536]{2,1,0:T(8,128)(2,1)} fusion(bf16[32,64,3072]{2,1,0:T(8,128)(2,1)} %all-gather.4.cloned.1.call-done, s32[]{:T(128)S(6)} %select_n.25, pred[]{:T(512)S(6)} %eq.18), kind=kLoop, calls=%fused_computation.19 | loop fusion | flops 3145728 | bytes 12582917 | tf_op jit(solution)/shard_map/jit(_where)/select_n | solution.py:10
  90.9 0.0 all-gather.6.cloned.1.call-update
  90.9 0.0 reduce-scatter.4.cloned.1.call-start
  91.0 0.0 copy-done.1
  91.0 0.7 fusion.20
  91.7 0.0 copy-done.3
  91.7 0.6 divide_bitcast_fusion
  92.3 423.9 %all-gather.6.cloned.1.call-done = bf16[128,64,1536]{2,1,0:T(8,128)(2,1)} async-done(((bf16[32,64,1536]{2,1,0:T(8,128)(2,1)}), bf16[128,64,1536]{2,1,0:T(8,128)(2,1)}) %all-gather.6.cloned.1.call-update) | async-done | bytes 25165840 | tf_op jit(solution)/shard_map/all_gather | solution.py:11
  516.2 17.7 %reduce_sum.39 = bf16[32,64,1536]{2,1,0:T(8,128)(2,1)} reduce(bf16[4,32,64,1536]{3,2,1,0:T(8,128)(2,1)} %bitcast.17, bf16[]{:T(256)} %constant.44.clone.1), dimensions={0}, to_apply=%region_0.1 | reduce | flops 9437184 | bytes 31457282 | tf_op jit(solution)/shard_map/reduce_sum | solution.py:11
  533.9 37.5 %fusion = bf16[2048]{0:T(1024)(128)(2,1)S(1)} fusion(bf16[2048,3072]{1,0:T(8,128)(2,1)} %bitcast.21, bf16[2048,1536]{1,0:T(8,128)(2,1)} %bitcast.18, f32[]{:T(128)} %bitcast.3, f32[1536,3072]{1,0:T(8,128)} %param.5, s32[3072]{0:T(1024)S(1)} %iota_add_fusion, s32[1536]{0:T(1024)S(1)} %iota_add_fusion.1, f32[1536,3072]{1,0:T(8,128)} %param.6), kind=kOutput, calls=%fused_computation.8 | convolution fusion | flops 19421722624 | bytes 56645636 | tf_op jit(solution)/shard_map/dot_general | solution.py:42
  571.4 0.7 stack.12
  572.1 37.7 %fusion.1 = bf16[2048]{0:T(1024)(128)(2,1)S(1)} fusion(bf16[2048,3072]{1,0:T(8,128)(2,1)} %bitcast.22, bf16[2048,1536]{1,0:T(8,128)(2,1)} %bitcast.19, f32[]{:T(128)} %bitcast.5, f32[1536,3072]{1,0:T(8,128)} %param.5, s32[3072]{0:T(1024)S(1)} %iota_add_fusion, s32[1536]{0:T(1024)S(1)} %iota_add_fusion.1, f32[1536,3072]{1,0:T(8,128)} %param.6), kind=kOutput, calls=%fused_computation.9 | convolution fusion | flops 19421722624 | bytes 56645636 | tf_op jit(solution)/shard_map/dot_general | solution.py:42
  609.8 0.1 stack.13
  609.9 0.0 copy-start
  609.9 0.0 copy-start.2
  609.9 37.8 %fusion.2 = bf16[2048]{0:T(1024)(128)(2,1)S(1)} fusion(bf16[2048,3072]{1,0:T(8,128)(2,1)} %bitcast.23, bf16[2048,1536]{1,0:T(8,128)(2,1)} %bitcast.20, f32[]{:T(128)} %bitcast.7, f32[1536,3072]{1,0:T(8,128)} %param.5, s32[3072]{0:T(1024)S(1)} %iota_add_fusion, s32[1536]{0:T(1024)S(1)} %iota_add_fusion.1, f32[1536,3072]{1,0:T(8,128)} %param.6), kind=kOutput, calls=%fused_computation.10 | convolution fusion | flops 19421722624 | bytes 56645636 | tf_op jit(solution)/shard_map/dot_general | solution.py:42
  647.7 0.1 stack.14
  647.7 0.0 copy-done
  647.8 0.0 copy-done.2
  647.8 0.1 fusion.12
  647.9 0.7 copy.8
  648.6 0.0 reduce-scatter.4.cloned.1.call-update
  648.6 17.6 %reduce-scatter.4.cloned.1.call-done = f32[16,3]{1,0:T(8,128)} async-done(((f32[64,3]{1,0:T(8,128)}), f32[16,3]{1,0:T(8,128)}) %reduce-scatter.4.cloned.1.call-update) | async-done | bytes 208
  666.2 0.8 copy.9
  667.0 12.4 %psum.7 = f32[3,16]{1,0:T(4,128)} all-reduce(f32[3,16]{1,0:T(4,128)S(1)} %copy.9), channel_id=1, replica_groups=mesh['grow'=8,'gcol'=4] {'grow'}, use_global_device_ids=true, to_apply=%region_5.6 | all-reduce | flops 48 | bytes 384 | tf_op jit(solution)/shard_map/psum | solution.py:49
  (3 shorter events, 0.0 us)
Async XLA Ops:
  6.5 84.5 %copy-start.1 = (f32[3]{0:T(128)S(1)}, f32[3]{0:T(128)}, u32[]{:S(2)}) copy-start(f32[3]{0:T(128)} %param.7) | copy-start | bytes 40
  6.5 85.1 %copy-start.3 = (f32[32]{0:T(128)S(1)}, f32[32]{0:T(128)}, u32[]{:S(2)}) copy-start(f32[32]{0:T(128)} %param.8) | copy-start | bytes 388
  6.5 77.4 %all-gather.4.cloned.1.call-start = ((), (), s32[]{:S(2)}) async-start(), calls=%async_computation.1 | async-start | bytes 14155776 | tf_op jit(solution)/shard_map/all_gather | solution.py:24
  7.3 509.0 %all-gather.6.cloned.1.call-start = ((), (), s32[]{:S(2)}) async-start(), calls=%async_computation.2 | async-start | bytes 31457280 | tf_op jit(solution)/shard_map/all_gather | solution.py:11
  90.9 575.2 %reduce-scatter.4.cloned.1.call-start = ((), (), s32[]{:S(2)}) async-start(), calls=%async_computation.3 | async-start | bytes 40960
  609.9 37.9 %copy-start = (bf16[1,32,64]{2,1,0:T(8,128)(2,1)S(1)}, bf16[1,32,64]{2,1,0:T(8,128)(2,1)}, u32[]{:S(2)}) copy-start(bf16[1,32,64]{2,1,0:T(8,128)(2,1)} %stack.12) | copy-start | bytes 12292
  609.9 37.9 %copy-start.2 = (bf16[3,32,1]{1,0,2:T(4,128)(2,1)S(1)}, bf16[3,32,1]{1,0,2:T(4,128)(2,1)}, u32[]{:S(2)}) copy-start(bf16[3,32,1]{1,0,2:T(4,128)(2,1)} %divide_bitcast_fusion) | copy-start | bytes 580
Sparse Core Ops, SparseCore 0:
  9.2 74.7 all-gather.3
  91.1 425.1 all-gather.5
  648.7 17.3 reduce-scatter.3
